TPU v7x, 8 devices: a whole 2x2x1 slice. The times are simulated.
8 devices in a mesh: dp: 8 (over z, y, x, core).
Axes of the slice: x: 2, y: 2, z: 1, core: 2. Of those that a mesh axis runs over, the one named last changes fastest.
Arguments:
- local_grads: bfloat16 [8, 32768, 1024], P('dp')
- master: float32 [32768, 1024], P('dp')
- mom_first: float32 [32768, 1024], P('dp')
- mom_second: float32 [32768, 1024], P('dp')
- learn_rate: float32 [], replicated
Outputs:
- output 1: float32 [32768, 1024], P('dp')
- output 2: float32 [32768, 1024], P('dp')
- output 3: float32 [32768, 1024], P('dp')
- output 4: bfloat16 [32768, 1024], replicated
All inputs are finite; a program needn't handle non-finite values.
Results may differ from a plain program's by a relative error of at most 0.001.
Values are sent between devices in bfloat16 or wider.
A program may use at most 1 GiB of HBM per device.

v0:
```python
import jax
import jax.numpy as jnp
from jax import lax
from jax.sharding import PartitionSpec as P, NamedSharding

LAYERS = 2
MIX_RANK = 32
DECAY_RANK = 64
ADAM_STEP = 10


def layout_runs(model_width, total_rows):
    ffn_width = 7 * model_width // 2
    layer_rows = 6 * model_width + 2 * ffn_width + 16 + 10 * MIX_RANK + 2 * DECAY_RANK
    vocab_rows = (total_rows - LAYERS * layer_rows - 4) // 2
    base_rule = (1.0, 0.0)
    decay_rule = (1.0, 0.1)
    time_rule = (2.0, 0.0)
    pieces = [(vocab_rows, decay_rule)]
    for layer_idx in range(LAYERS):
        lead_rows = 12 if layer_idx == 0 else 10
        pieces = pieces + [(lead_rows + 10 * MIX_RANK, base_rule), (1, time_rule), (2 * DECAY_RANK, base_rule), (1, time_rule), (5 * model_width, decay_rule), (4, base_rule), (2 * ffn_width + model_width, decay_rule)]
    pieces = pieces + [(2, base_rule), (vocab_rows, decay_rule)]
    run_starts = []
    next_row = 0
    for run_len, run_rule in pieces:
        run_starts.append(next_row)
        next_row = next_row + run_len
    lr_values = [run_rule[0] for run_len, run_rule in pieces]
    decay_values = [run_rule[1] for run_len, run_rule in pieces]
    return run_starts, lr_values, decay_values


def row_rules(row_ids, model_width, total_rows):
    run_starts, lr_values, decay_values = layout_runs(model_width, total_rows)
    later_starts = jnp.asarray(run_starts[1:], jnp.int32)
    run_index = jnp.sum((row_ids[:, None] >= later_starts[None, :]).astype(jnp.int32), axis=1)
    lr_factor = jnp.asarray(lr_values, jnp.float32)[run_index]
    decay_rate = jnp.asarray(decay_values, jnp.float32)[run_index]
    return lr_factor[:, None], decay_rate[:, None]


def adam_rows(grad_rows, master_rows, first_rows, second_rows, clip_scale, learn_rate, lr_factor, decay_rate):
    clipped = grad_rows * clip_scale
    new_first = 0.9 * first_rows + 0.1 * clipped
    new_second = 0.99 * second_rows + 0.01 * (clipped * clipped)
    first_hat = new_first / (1.0 - 0.9 ** ADAM_STEP)
    second_hat = new_second / (1.0 - 0.99 ** ADAM_STEP)
    step_size = learn_rate * lr_factor
    new_master = master_rows - step_size * (first_hat / (jnp.sqrt(second_hat) + 1e-8) + decay_rate * master_rows)
    return new_master, new_first, new_second


def solution(mesh):
    dev_count = mesh.shape['dp']

    def device_step(local_grads, master, mom_first, mom_second, learn_rate):
        shard_rows = master.shape[0]
        model_width = master.shape[1]
        total_rows = shard_rows * dev_count
        grad_shard = lax.psum_scatter(local_grads[0].astype(jnp.float32), 'dp', scatter_dimension=0, tiled=True) / dev_count
        square_sum = lax.psum(jnp.sum(grad_shard * grad_shard), 'dp')
        clip_scale = jnp.minimum(1.0, 1.0 / (jnp.sqrt(square_sum) + 1e-6))
        row_ids = lax.axis_index('dp') * shard_rows + lax.iota(jnp.int32, shard_rows)
        lr_factor, decay_rate = row_rules(row_ids, model_width, total_rows)
        new_master, new_first, new_second = adam_rows(grad_shard, master, mom_first, mom_second, clip_scale, learn_rate, lr_factor, decay_rate)
        working = lax.all_gather(new_master.astype(jnp.bfloat16), 'dp', axis=0, tiled=True)
        return new_master, new_first, new_second, working

    return jax.shard_map(device_step, mesh=mesh, in_specs=(P('dp', None, None), P('dp', None), P('dp', None), P('dp', None), P()), out_specs=(P('dp', None), P('dp', None), P('dp', None), P(None, None)), check_vma=False)
```

profile of v0, /device:TPU:0, one launch (start us, length us, event | category | flops | bytes accessed | tf_op | source)
XLA Modules:
  0.0 1238.7 jit_solution(1611782544533086294)
XLA Ops:
  7.2 0.0 reduce-scatter.2.cloned.1.call-start
  7.2 66.2 %bitcast_convert_fusion = f32[32768,1024]{1,0:T(8,128)} fusion(bf16[1,32768,1024]{2,1,0:T(8,128)(2,1)} %param.8), kind=kLoop, calls=%fused_computation | loop fusion | flops 33554432 | bytes 201326592 | tf_op jit(solution)/shard_map/convert_element_type | solution.py:61
  73.4 0.0 copy-start
  73.4 0.0 reduce-scatter.2.cloned.1.call-update
  73.4 0.0 all-gather.2.cloned.1.call-start
  74.1 0.0 copy-done
  74.1 0.1 convert_reduce_fusion
  74.3 0.1 compare_select_fusion.2
  74.3 0.5 compare_reduce_fusion.9
  74.8 0.1 compare_select_fusion.3
  74.9 733.4 %reduce-scatter.2.cloned.1.call-done = f32[4096,1024]{1,0:T(8,128)} async-done(((f32[32768,1024]{1,0:T(8,128)}), f32[4096,1024]{1,0:T(8,128)}) %reduce-scatter.2.cloned.1.call-update) | async-done | bytes 16777232 | tf_op jit(solution)/shard_map/reduce_scatter | solution.py:61
  808.2 10.7 multiply_reduce_fusion
  819.0 22.5 %psum.7 = f32[]{:T(128)} all-reduce(f32[]{:T(128)} %multiply_reduce_fusion), channel_id=1, replica_groups=mesh['dp'=8] {'dp'}, use_global_device_ids=true, to_apply=%region_3.0 | all-reduce | flops 1 | bytes 8 | tf_op jit(solution)/shard_map/psum | solution.py:62
  842.2 46.1 %fusion = (bf16[4096,1024]{1,0:T(8,128)(2,1)}, f32[4096,1024]{1,0:T(8,128)}, f32[4096,1024]{1,0:T(8,128)}, f32[4096,1024]{1,0:T(8,128)}) fusion(f32[4096,1024]{1,0:T(8,128)} %param.9, f32[4096]{0:T(1024)S(1)} %get-tuple-element.21, f32[4096]{0:T(1024)S(1)} %get-tuple-element.20, f32[4096,1024]{1,0:T(8,128)} %reduce-scatter.2.cloned.1.call-done, f32[]{:T(128)S(6)} %mul.75, ...), kind=kLoop, calls=%fused_computation.31 | loop fusion | flops 71303168 | bytes 125861888 | tf_op jit(solution)/shard_map/convert_element_type | solution.py:67
  888.2 0.0 all-gather.2.cloned.1.call-update
  888.3 299.3 %all-gather.2.cloned.1.call-done = bf16[32768,1024]{1,0:T(8,128)(2,1)} async-done(((bf16[4096,1024]{1,0:T(8,128)(2,1)}), bf16[32768,1024]{1,0:T(8,128)(2,1)}) %all-gather.2.cloned.1.call-update) | async-done | bytes 67108880 | tf_op jit(solution)/shard_map/all_gather | solution.py:67
  1187.5 44.3 %copy.14 = bf16[32768,1024]{1,0:T(8,128)(2,1)} copy(bf16[32768,1024]{1,0:T(8,128)(2,1)} %all-gather.2.cloned.1.call-done) | data formatting | bytes 134217728
  (2 shorter events, 0.0 us)
Async XLA Ops:
  7.2 801.1 %reduce-scatter.2.cloned.1.call-start = ((), (), s32[]{:S(2)}) async-start(), calls=%async_computation.1 | async-start | bytes 150994944 | tf_op jit(solution)/shard_map/reduce_scatter | solution.py:61
  73.4 0.7 copy-start
  73.4 1114.1 %all-gather.2.cloned.1.call-start = ((), (), s32[]{:S(2)}) async-start(), calls=%async_computation.2 | async-start | bytes 75497472 | tf_op jit(solution)/shard_map/all_gather | solution.py:67
Sparse Core Ops, SparseCore 0:
  73.5 734.6 reduce-scatter.1
  888.4 299.1 all-gather.1
where the time goes:
time: 1240 us
  waiting for transfers between devices  1030 us (83%)
  other arithmetic  124 us (10%)
  local copies, waits for them, and re-layouts  44.3 us (4%)
  blocking collectives  22.5 us (2%)
  between operations  15.5 us (1%)
    reduce_scatter x1, waiting for transfers between devices, device_step(): lax.psum_scatter(local_grads[0].astype(jnp.float32), 'dp', scatter_dimens...  733 us
    all_gather x1, waiting for transfers between devices, device_step(): lax.all_gather(new_master.astype(jnp.bfloat16), 'dp', axis=0, tiled=True)  299 us
    convert_element_type x1, other arithmetic, device_step(): local_grads[0].astype(jnp.float32)  66.2 us
    convert_element_type x1, other arithmetic, device_step(): new_master.astype(jnp.bfloat16)  46.1 us
    unnamed x3, local copies, waits for them, and re-layouts  44.3 us
  transfers between devices with their start and end apart: 2, of which 2 were waited for; matrix products, arithmetic and copies ran while one was open for 0% of the time, Pallas kernels for 0%

commit v1 on v0

v1 whole, which is shorter than its diff:
```python
import functools

import jax
import jax.numpy as jnp
from jax import lax
from jax.experimental import pallas as pl
from jax.experimental.pallas import tpu as pltpu
from jax.sharding import PartitionSpec as P

LAYERS = 2
MIX_RANK = 32
DECAY_RANK = 64
ADAM_STEP = 10

MESH = pl.DeviceIdType.MESH
CHUNK = 256
DIRECT = 1024
GROUP = 16
BLOCK = 256
PARTS = (512, 1536, 1536, 512)


def layout_runs(model_width, total_rows):
    ffn_width = 7 * model_width // 2
    layer_rows = 6 * model_width + 2 * ffn_width + 16 + 10 * MIX_RANK + 2 * DECAY_RANK
    vocab_rows = (total_rows - LAYERS * layer_rows - 4) // 2
    base_rule = (1.0, 0.0)
    decay_rule = (1.0, 0.1)
    time_rule = (2.0, 0.0)
    pieces = [(vocab_rows, decay_rule)]
    for layer_idx in range(LAYERS):
        lead_rows = 12 if layer_idx == 0 else 10
        pieces = pieces + [(lead_rows + 10 * MIX_RANK, base_rule), (1, time_rule), (2 * DECAY_RANK, base_rule), (1, time_rule), (5 * model_width, decay_rule), (4, base_rule), (2 * ffn_width + model_width, decay_rule)]
    pieces = pieces + [(2, base_rule), (vocab_rows, decay_rule)]
    runs = []
    next_row = 0
    for run_len, run_rule in pieces:
        runs.append((next_row, run_rule[0], run_rule[1]))
        next_row = next_row + run_len
    return runs


def reduce_kernel(half, grads, total, clip, rx, pd, p2, stage, own, other, near0, near1, last, result, squares, norms,
                  p1_send, direct_send, pair_send, p2_send, norm_send, rx_sem, direct_sem, pair_sem, p2_sem, norm_sem, load_sem, store_sem):
    me = lax.axis_index("dp")
    count = 8
    core = lax.rem(me, 2)
    chip = lax.div(me, 2)
    x, y = lax.rem(chip, 2), lax.div(chip, 2)
    x_near, y_near = y * 2 + 1 - x, (1 - y) * 2 + x
    diagonal = (1 - y) * 2 + 1 - x
    first = (x_near, y_near)
    second = (y_near, x_near)
    partner = chip * 2 + 1 - core
    chunks = half // CHUNK
    directs = half // DIRECT

    barrier = pltpu.get_barrier_semaphore()
    for step in range(1, count):
        pl.semaphore_signal(barrier, inc=1, device_id=(lax.rem(me + step, count),), device_id_type=MESH)
    pl.semaphore_wait(barrier, count - 1)

    def forward_copy(h, to_core, k):
        rows = pl.ds(h * half + k * CHUNK, CHUNK)
        return pltpu.make_async_remote_copy(
            src_ref=grads.at[diagonal * 2 + to_core, rows], dst_ref=rx.at[h, 0, core, pl.ds(k * CHUNK, CHUNK)],
            send_sem=p1_send.at[h, to_core, k], recv_sem=rx_sem.at[h, core, k],
            device_id=(first[h] * 2 + to_core,), device_id_type=MESH)

    def direct_copy(h, to_core, k):
        rows = pl.ds(h * half + k * DIRECT, DIRECT)
        return pltpu.make_async_remote_copy(
            src_ref=grads.at[first[h] * 2 + to_core, rows], dst_ref=rx.at[h, 1, core, pl.ds(k * DIRECT, DIRECT)],
            send_sem=direct_send.at[h, to_core, k], recv_sem=direct_sem.at[h, core, k],
            device_id=(first[h] * 2 + to_core,), device_id_type=MESH)

    def pair_copy(h, kind):
        owner = (second[h] if kind == 0 else chip) * 2 + 1 - core
        return pltpu.make_async_remote_copy(
            src_ref=grads.at[owner, pl.ds(h * half, half)], dst_ref=pd.at[h, kind],
            send_sem=pair_send.at[h, kind], recv_sem=pair_sem.at[h, kind],
            device_id=(partner,), device_id_type=MESH)

    def second_copy(h, k):
        rows = pl.ds(k * CHUNK, CHUNK)
        return pltpu.make_async_remote_copy(
            src_ref=stage.at[h, rows], dst_ref=p2.at[h, rows],
            send_sem=p2_send.at[h, k], recv_sem=p2_sem.at[h, k],
            device_id=(second[h] * 2 + core,), device_id_type=MESH)

    for k in range(chunks):
        for h in range(2):
            for to_core in range(2):
                forward_copy(h, to_core, k).start()
        if k == 0:
            for h in range(2):
                pair_copy(h, 0).start()
        if k == 2:
            for h in range(2):
                pair_copy(h, 1).start()
    for k in range(directs):
        for h in range(2):
            for to_core in range(2):
                direct_copy(h, to_core, k).start()

    def loads(h, kind, k):
        owner = (second[h] if kind == 0 else chip) * 2 + core
        rows = pl.ds(k * CHUNK, CHUNK)
        copies = [
            pltpu.make_async_copy(grads.at[owner, pl.ds(h * half + k * CHUNK, CHUNK)], own, load_sem.at[0]),
            pltpu.make_async_copy(pd.at[h, kind, rows], other, load_sem.at[1]),
            pltpu.make_async_copy(rx.at[h, kind, 0, rows], near0, load_sem.at[2]),
            pltpu.make_async_copy(rx.at[h, kind, 1, rows], near1, load_sem.at[3]),
        ]
        if kind == 1:
            copies.append(pltpu.make_async_copy(p2.at[h, rows], last, load_sem.at[4]))
        for copy in copies:
            copy.start()
        for copy in copies:
            copy.wait()

    def four(rows):
        return (own[rows].astype(jnp.float32) + other[rows].astype(jnp.float32)) + (near0[rows].astype(jnp.float32) + near1[rows].astype(jnp.float32))

    for h in range(2):
        pair_copy(h, 0).wait_recv()

    def forward_step(k, carry):
        for h in range(2):
            for from_core in range(2):
                pltpu.make_async_copy(rx.at[h, 0, from_core, pl.ds(0, CHUNK)], rx.at[h, 0, from_core, pl.ds(0, CHUNK)], rx_sem.at[h, from_core, k]).wait()
            loads(h, 0, k)

            def add(group, carry):
                base = pl.multiple_of(group * GROUP, GROUP)
                stage[h, pl.ds(pl.multiple_of(k * CHUNK + base, GROUP), GROUP)] = four(pl.ds(base, GROUP))
                return carry

            lax.fori_loop(0, CHUNK // GROUP, add, 0)
            second_copy(h, k).start()
        return carry

    lax.fori_loop(0, chunks, forward_step, 0)

    for h in range(2):
        pair_copy(h, 1).wait_recv()
        for from_core in range(2):
            for k in range(directs):
                rows = pl.ds(k * DIRECT, DIRECT)
                pltpu.make_async_copy(rx.at[h, 1, from_core, rows], rx.at[h, 1, from_core, rows], direct_sem.at[h, from_core, k]).wait()

    squares[...] = jnp.zeros_like(squares)

    def owner_step(k, carry):
        for h in range(2):
            second_copy(h, k).wait_recv()
            loads(h, 1, k)

            def add(group, carry):
                rows = pl.ds(pl.multiple_of(group * GROUP, GROUP), GROUP)
                mean = (four(rows) + last[rows]) * (1.0 / count)
                result[rows] = mean
                squares[...] += mean * mean
                return carry

            lax.fori_loop(0, CHUNK // GROUP, add, 0)
            store = pltpu.make_async_copy(result, total.at[pl.ds(h * half + k * CHUNK, CHUNK)], store_sem.at[0])
            store.start()
            store.wait()
        return carry

    lax.fori_loop(0, chunks, owner_step, 0)

    lanes = jnp.sum(squares[...].reshape(GROUP // 8, 8, squares.shape[1]), axis=0)
    partial = lanes[:, 0:128]
    for column in range(1, squares.shape[1] // 128):
        partial += lanes[:, column * 128:(column + 1) * 128]
    norms[me] = partial

    for h in range(2):
        for to_core in range(2):
            for k in range(chunks):
                forward_copy(h, to_core, k).wait_send()
            for k in range(directs):
                direct_copy(h, to_core, k).wait_send()
        for kind in range(2):
            pair_copy(h, kind).wait_send()
        for k in range(chunks):
            second_copy(h, k).wait_send()

    def norm_copy(step):
        to = lax.rem(me + step, count)
        return pltpu.make_async_remote_copy(
            src_ref=norms.at[me], dst_ref=norms.at[me], send_sem=norm_send.at[step], recv_sem=norm_sem.at[me],
            device_id=(to,), device_id_type=MESH)

    for step in range(1, count):
        norm_copy(step).start()
    for step in range(1, count):
        source = lax.rem(me + step, count)
        pltpu.make_async_copy(norms.at[source], norms.at[source], norm_sem.at[source]).wait()
    for step in range(1, count):
        norm_copy(step).wait_send()
    square_sum = jnp.sum(jnp.sum(norms[...], axis=0))
    norm = jnp.sqrt(jnp.full(clip.shape, square_sum, jnp.float32))
    clip[...] = jnp.minimum(1.0, 1.0 / (norm + 1e-6))


def reduce_gradients(local_grads, count):
    _, total_rows, width = local_grads.shape
    rows = total_rows // count
    half = rows // 2
    chunks, directs = half // CHUNK, half // DIRECT
    any_space = pl.BlockSpec(memory_space=pl.ANY)
    outs = pl.pallas_call(
        functools.partial(reduce_kernel, half),
        name="reduce_gradients",
        out_shape=(
            jax.ShapeDtypeStruct((rows, width), jnp.float32),
            jax.ShapeDtypeStruct((8, 128), jnp.float32),
            jax.ShapeDtypeStruct((2, 2, 2, half, width), jnp.bfloat16),
            jax.ShapeDtypeStruct((2, 2, half, width), jnp.bfloat16),
            jax.ShapeDtypeStruct((2, half, width), jnp.float32),
        ),
        in_specs=[any_space],
        out_specs=(any_space, pl.BlockSpec(memory_space=pltpu.VMEM), any_space, any_space, any_space),
        scratch_shapes=[
            pltpu.VMEM((2, half, width), jnp.float32),
            pltpu.VMEM((CHUNK, width), jnp.bfloat16),
            pltpu.VMEM((CHUNK, width), jnp.bfloat16),
            pltpu.VMEM((CHUNK, width), jnp.bfloat16),
            pltpu.VMEM((CHUNK, width), jnp.bfloat16),
            pltpu.VMEM((CHUNK, width), jnp.float32),
            pltpu.VMEM((CHUNK, width), jnp.float32),
            pltpu.VMEM((GROUP, width), jnp.float32),
            pltpu.VMEM((count, 8, 128), jnp.float32),
            pltpu.SemaphoreType.DMA((2, 2, chunks)),
            pltpu.SemaphoreType.DMA((2, 2, directs)),
            pltpu.SemaphoreType.DMA((2, 2)),
            pltpu.SemaphoreType.DMA((2, chunks)),
            pltpu.SemaphoreType.DMA((count,)),
            pltpu.SemaphoreType.DMA((2, 2, chunks)),
            pltpu.SemaphoreType.DMA((2, 2, directs)),
            pltpu.SemaphoreType.DMA((2, 2)),
            pltpu.SemaphoreType.DMA((2, chunks)),
            pltpu.SemaphoreType.DMA((count,)),
            pltpu.SemaphoreType.DMA((5,)),
            pltpu.SemaphoreType.DMA((1,)),
        ],
        compiler_params=pltpu.CompilerParams(collective_id=0, has_side_effects=True, vmem_limit_bytes=60 * 1024 * 1024),
    )(local_grads.reshape(count, rows, width))
    return outs[0], outs[1]


def update_kernel(start, shard_rows, runs, has_state, learn_rate, clip, grad, master, first, second, *refs):
    new_master, new_first, new_second, working = refs[3:7] if has_state else refs[0:4]
    block = grad.shape[0]
    base = lax.axis_index("dp") * shard_rows + start + pl.program_id(0) * block
    row = base + lax.broadcasted_iota(jnp.int32, (block, 128), 0)
    factor = jnp.full((block, 128), runs[0][1], jnp.float32)
    decay = jnp.full((block, 128), runs[0][2], jnp.float32)
    for before, run in zip(runs[:-1], runs[1:]):
        later = row >= run[0]
        if run[1] != before[1]:
            factor = jnp.where(later, run[1], factor)
        if run[2] != before[2]:
            decay = jnp.where(later, run[2], decay)
    step_size = learn_rate[0] * factor
    scale = clip[0:1, :]
    for column in range(grad.shape[1] // 128):
        lanes = pl.ds(column * 128, 128)
        clipped = grad[:, lanes] * scale
        first_value = 0.9 * first[:, lanes] + 0.1 * clipped
        second_value = 0.99 * second[:, lanes] + 0.01 * (clipped * clipped)
        first_hat = first_value * (1.0 / (1.0 - 0.9 ** ADAM_STEP))
        second_hat = second_value * (1.0 / (1.0 - 0.99 ** ADAM_STEP))
        old = master[:, lanes]
        value = old - step_size * (first_hat / (jnp.sqrt(second_hat) + 1e-8) + decay * old)
        new_master[:, lanes] = value
        new_first[:, lanes] = first_value
        new_second[:, lanes] = second_value
        working[:, lanes] = value.astype(jnp.bfloat16)


def update_rows(start, rows, runs, state, gathered_shape, learn_rate, clip, grad, master, first, second):
    shard_rows, width = grad.shape
    block = pl.BlockSpec((BLOCK, width), lambda i: (start // BLOCK + i, 0))
    any_space = pl.BlockSpec(memory_space=pl.ANY)
    in_specs = [pl.BlockSpec(memory_space=pltpu.SMEM), pl.BlockSpec((8, 128), lambda i: (0, 0)), block, block, block, block]
    args = [learn_rate, clip, grad, master, first, second]
    aliases = {}
    if state is not None:
        aliases = {len(args) + i: i for i in range(3)}
        in_specs += [any_space] * 3
        args += list(state)
    whole = jax.ShapeDtypeStruct((shard_rows, width), jnp.float32)
    out_shape = [whole, whole, whole, jax.ShapeDtypeStruct((rows, width), jnp.bfloat16)]
    out_specs = [block, block, block, pl.BlockSpec((BLOCK, width), lambda i: (i, 0))]
    if gathered_shape is not None:
        out_shape.append(gathered_shape)
        out_specs.append(any_space)
    size = rows * width
    return pl.pallas_call(
        functools.partial(update_kernel, start, shard_rows, runs, state is not None),
        name="update_rows",
        grid=(rows // BLOCK,),
        out_shape=tuple(out_shape),
        in_specs=in_specs,
        out_specs=tuple(out_specs),
        input_output_aliases=aliases,
        cost_estimate=pl.CostEstimate(flops=20 * size, bytes_accessed=30 * size, transcendentals=2 * size),
        compiler_params=pltpu.CompilerParams(dimension_semantics=("arbitrary",), vmem_limit_bytes=48 * 1024 * 1024),
    )(*args)


def place_kernel(gathered, working_in, working):
    working[...] = gathered[0]


def place_rows(start, working, gathered):
    count, rows, width = gathered.shape
    shard_rows = working.shape[0] // count
    size = rows * width * count
    return pl.pallas_call(
        place_kernel,
        name="place_rows",
        grid=(count, rows // 512),
        out_shape=jax.ShapeDtypeStruct(working.shape, working.dtype),
        in_specs=[pl.BlockSpec((1, 512, width), lambda d, i: (d, i, 0)), pl.BlockSpec(memory_space=pl.ANY)],
        out_specs=pl.BlockSpec((512, width), lambda d, i: (d * (shard_rows // 512) + start // 512 + i, 0)),
        input_output_aliases={1: 0},
        cost_estimate=pl.CostEstimate(flops=size, bytes_accessed=4 * size, transcendentals=0),
        compiler_params=pltpu.CompilerParams(dimension_semantics=("arbitrary", "arbitrary")),
    )(gathered, working)


def solution(mesh):
    count = mesh.shape["dp"]

    def device_step(local_grads, master, mom_first, mom_second, learn_rate):
        shard_rows, width = master.shape
        total_rows = shard_rows * count
        runs = layout_runs(width, total_rows)
        grad, clip = reduce_gradients(local_grads, count)
        rate = learn_rate.reshape(1)
        state = None
        start = 0
        gathered = []
        for index, rows in enumerate(PARTS):
            shape = jax.ShapeDtypeStruct((total_rows, width), jnp.bfloat16) if index == len(PARTS) - 1 else None
            outs = update_rows(start, rows, runs, state, shape, rate, clip, grad, master, mom_first, mom_second)
            state = outs[0:3]
            gathered.append((start, lax.all_gather(outs[3], "dp", axis=0, tiled=False)))
            start += rows
        working = outs[4]
        for start, block in gathered:
            working = place_rows(start, working, block)
        return state[0], state[1], state[2], working

    return jax.shard_map(device_step, mesh=mesh, in_specs=(P("dp", None, None), P("dp", None), P("dp", None), P("dp", None), P()), out_specs=(P("dp", None), P("dp", None), P("dp", None), P(None, None)), check_vma=False)
```

time: 1240 us -> 931 us (0.75)
  waiting for transfers between devices: 1030 us -> 240 us
  Pallas kernels: 0 us -> 674 us
  other arithmetic: 124 us -> 0 us
  local copies, waits for them, and re-layouts: 44.3 us -> 0.68 us
  blocking collectives: 22.5 us -> 0 us
    reduce_scatter x1 -> x0, waiting for transfers between devices: 733 us -> none  [device_step(): lax.psum_scatter(local_grads[0].astype(jnp.float32), 'dp', scatter_dimens...]
    pallas_call x0 -> x9, Pallas kernels: none -> 674 us  [the longest x1 557 us: reduce_gradients(): pl.pallas_call(functools.partial(reduce_kernel, half), name='reduce_gradi...]
    convert_element_type x2 -> x0, other arithmetic: 112 us -> none  [the longest x1 66.2 us: device_step(): local_grads[0].astype(jnp.float32)]
    all_gather x1 -> x4, waiting for transfers between devices: 299 us -> 240 us  [device_step(): gathered.append((start, lax.all_gather(outs[3], 'dp', axis=0, tiled=False)))]
    unnamed x3 -> x4, local copies, waits for them, and re-layouts: 44.3 us -> 0.68 us
    psum x1 -> x0, blocking collectives: 22.5 us -> none  [device_step(): square_sum = lax.psum(jnp.sum(grad_shard * grad_shard), 'dp')]
  transfers between devices with their start and end apart: 2 -> 4, of which waited for: 2 -> 4; matrix products, arithmetic and copies ran while one was open for 0% -> 0% of each run, Pallas kernels for 0% -> 11%
where the time goes in v1:
time: 931 us; the launch traced here: 929 us
  Pallas kernels  674 us (72%)
  waiting for transfers between devices  240 us (26%)
  between operations  14.4 us (2%)
    pallas_call x1, Pallas kernels, reduce_gradients(): pl.pallas_call(functools.partial(reduce_kernel, half), name='reduce_gradi...  557 us
    all_gather x4, waiting for transfers between devices, device_step(): gathered.append((start, lax.all_gather(outs[3], 'dp', axis=0, tiled=False)))  240 us
    pallas_call x4, Pallas kernels, place_rows(): pl.pallas_call(place_kernel, name='place_rows', grid=(count, rows // 512)...  69.8 us
    pallas_call x4, Pallas kernels, update_rows(): pl.pallas_call(functools.partial(update_kernel, start, shard_rows, runs,...  47.1 us
  transfers between devices with their start and end apart: 4, of which 4 were waited for; matrix products, arithmetic and copies ran while one was open for 0% of the time, Pallas kernels for 11%

profile of v1, /device:TPU:0, one launch (start us, length us, event | category | flops | bytes accessed | tf_op | source)
XLA Modules:
  0.0 928.8 jit_solution(12066527587521558552)
XLA Ops:
  7.2 0.0 all-gather.15.cloned.1.call-start
  7.2 557.0 %reduce_gradients.1 = (f32[4096,1024]{1,0:T(8,128)}, f32[8,128]{1,0:T(8,128)}, bf16[2,2,2,2048,1024]{4,3,2,1,0:T(8,128)(2,1)}, bf16[2,2,2048,1024]{3,2,1,0:T(8,128)(2,1)}, f32[2,2048,1024]{2,1,0:T(8,128)}) custom-call(bf16[8,4096,1024]{2,1,0:T(8,128)(2,1)} %bitcast.1.grads), custom_call_target="tpu_custom_call" | custom-call | tf_op jit(solution)/shard_map/reduce_gradients/pallas_call | solution.py:215
  564.9 0.0 copy-start
  564.9 0.7 copy-done
  565.6 0.0 copy-start.1
  565.6 6.2 update_rows.4
  571.8 0.0 all-gather.15.cloned.1.call-update
  571.8 0.0 all-gather.13.cloned.1.call-start
  571.9 0.0 copy-done.1
  571.9 17.3 %update_rows.5 = (f32[4096,1024]{1,0:T(8,128)}, f32[4096,1024]{1,0:T(8,128)}, f32[4096,1024]{1,0:T(8,128)}, bf16[1536,1024]{1,0:T(8,128)(2,1)}) custom-call(f32[1]{0:T(128)} %bitcast.7.learn_rate, f32[8,128]{1,0:T(8,128)S(1)} %copy-done.1, f32[4096,1024]{1,0:T(8,128)} %get-tuple-element.24.grad, ...), custom_call_target="tpu_custom_call", output_to_operand_aliasing={{0}: (6, {}), {1}: (7, {}), {2}: (8, {})} | custom-call | flops 31457280 | bytes 47185920 | tf_op jit(solution)/shard_map/update_rows/pallas_call | solution.py:303
  589.2 0.0 all-gather.13.cloned.1.call-update
  589.2 0.0 all-gather.11.cloned.1.call-start
  589.3 17.3 %update_rows.6 = (f32[4096,1024]{1,0:T(8,128)}, f32[4096,1024]{1,0:T(8,128)}, f32[4096,1024]{1,0:T(8,128)}, bf16[1536,1024]{1,0:T(8,128)(2,1)}) custom-call(f32[1]{0:T(128)} %bitcast.8.learn_rate, f32[8,128]{1,0:T(8,128)S(1)} %copy-done.1, f32[4096,1024]{1,0:T(8,128)} %get-tuple-element.24.grad, ...), custom_call_target="tpu_custom_call", output_to_operand_aliasing={{0}: (6, {}), {1}: (7, {}), {2}: (8, {})} | custom-call | flops 31457280 | bytes 47185920 | tf_op jit(solution)/shard_map/update_rows/pallas_call | solution.py:303
  606.6 0.0 all-gather.11.cloned.1.call-update
  606.6 0.0 all-gather.9.cloned.1.call-start
  606.6 6.3 update_rows.7
  612.9 0.0 all-gather.9.cloned.1.call-update
  612.9 7.4 all-gather.15.cloned.1.call-done
  620.3 9.0 place_rows.4.working_in
  629.3 112.5 %all-gather.13.cloned.1.call-done = bf16[12288,1024]{1,0:T(8,128)(2,1)} async-done(((bf16[1536,1024]{1,0:T(8,128)(2,1)}), bf16[12288,1024]{1,0:T(8,128)(2,1)}) %all-gather.13.cloned.1.call-update) | async-done | bytes 25165840 | tf_op jit(solution)/shard_map/all_gather | solution.py:353
  741.8 25.9 %place_rows.5.working_in = bf16[32768,1024]{1,0:T(8,128)(2,1)} custom-call(bf16[8,1536,1024]{2,1,0:T(8,128)(2,1)} %bitcast.10, bf16[32768,1024]{1,0:T(8,128)(2,1)} %place_rows.4.working_in), custom_call_target="tpu_custom_call", output_to_operand_aliasing={{}: (1, {})} | custom-call | flops 12582912 | bytes 50331648 | tf_op jit(solution)/shard_map/place_rows/pallas_call | solution.py:324
  767.7 95.6 %all-gather.11.cloned.1.call-done = bf16[12288,1024]{1,0:T(8,128)(2,1)} async-done(((bf16[1536,1024]{1,0:T(8,128)(2,1)}), bf16[12288,1024]{1,0:T(8,128)(2,1)}) %all-gather.11.cloned.1.call-update) | async-done | bytes 25165840 | tf_op jit(solution)/shard_map/all_gather | solution.py:353
  863.3 25.9 %place_rows.6.working_in = bf16[32768,1024]{1,0:T(8,128)(2,1)} custom-call(bf16[8,1536,1024]{2,1,0:T(8,128)(2,1)} %bitcast.11, bf16[32768,1024]{1,0:T(8,128)(2,1)} %place_rows.5.working_in), custom_call_target="tpu_custom_call", output_to_operand_aliasing={{}: (1, {})} | custom-call | flops 12582912 | bytes 50331648 | tf_op jit(solution)/shard_map/place_rows/pallas_call | solution.py:324
  889.2 24.1 %all-gather.9.cloned.1.call-done = bf16[4096,1024]{1,0:T(8,128)(2,1)} async-done(((bf16[512,1024]{1,0:T(8,128)(2,1)}), bf16[4096,1024]{1,0:T(8,128)(2,1)}) %all-gather.9.cloned.1.call-update) | async-done | bytes 8388624 | tf_op jit(solution)/shard_map/all_gather | solution.py:353
  913.3 9.0 place_rows.7
Async XLA Ops:
  7.2 613.2 %all-gather.15.cloned.1.call-start = ((), (), s32[]{:S(2)}) async-start(), calls=%async_computation.3 | async-start | bytes 9437184 | tf_op jit(solution)/shard_map/all_gather | solution.py:353
  564.9 0.7 copy-start
  565.6 6.3 copy-start.1
  571.8 170.0 %all-gather.13.cloned.1.call-start = ((), (), s32[]{:S(2)}) async-start(), calls=%async_computation.2 | async-start | bytes 28311552 | tf_op jit(solution)/shard_map/all_gather | solution.py:353
  589.2 274.1 %all-gather.11.cloned.1.call-start = ((), (), s32[]{:S(2)}) async-start(), calls=%async_computation.1 | async-start | bytes 28311552 | tf_op jit(solution)/shard_map/all_gather | solution.py:353
  606.6 306.7 %all-gather.9.cloned.1.call-start = ((), (), s32[]{:S(2)}) async-start(), calls=%async_computation | async-start | bytes 9437184 | tf_op jit(solution)/shard_map/all_gather | solution.py:353
Sparse Core Ops, SparseCore 0:
  571.9 48.3 all-gather.14
  622.1 119.6 all-gather.12
  743.6 119.6 all-gather.10
  865.0 48.3 all-gather.8

commit v2 on v1

--- a/solution.py
+++ b/solution.py
@@ -17,7 +17,9 @@
 DIRECT = 1024
 GROUP = 16
 BLOCK = 256
-PARTS = (512, 1536, 1536, 512)
+PARTS = (512, 3072, 512)
+PIECE = 512
+DEPTH = 16
 
 
 def layout_runs(model_width, total_rows):
@@ -40,15 +42,17 @@
     return runs
 
 
-def reduce_kernel(half, grads, total, clip, rx, pd, p2, stage, own, other, near0, near1, last, result, squares, norms,
+def places(axis):
+    me = lax.axis_index(axis)
+    core, chip = lax.rem(me, 2), lax.div(me, 2)
+    x, y = lax.rem(chip, 2), lax.div(chip, 2)
+    return me, core, chip, y * 2 + 1 - x, (1 - y) * 2 + x, (1 - y) * 2 + 1 - x
+
+
+def reduce_kernel(half, grads, total, clip, rx, pd, stage, inbox, mine, own, other, near0, near1, squares, norms,
                   p1_send, direct_send, pair_send, p2_send, norm_send, rx_sem, direct_sem, pair_sem, p2_sem, norm_sem, load_sem, store_sem):
-    me = lax.axis_index("dp")
+    me, core, chip, x_near, y_near, diagonal = places("dp")
     count = 8
-    core = lax.rem(me, 2)
-    chip = lax.div(me, 2)
-    x, y = lax.rem(chip, 2), lax.div(chip, 2)
-    x_near, y_near = y * 2 + 1 - x, (1 - y) * 2 + x
-    diagonal = (1 - y) * 2 + 1 - x
     first = (x_near, y_near)
     second = (y_near, x_near)
     partner = chip * 2 + 1 - core
@@ -84,7 +88,7 @@
     def second_copy(h, k):
         rows = pl.ds(k * CHUNK, CHUNK)
         return pltpu.make_async_remote_copy(
-            src_ref=stage.at[h, rows], dst_ref=p2.at[h, rows],
+            src_ref=stage.at[h, rows], dst_ref=inbox.at[h, rows],
             send_sem=p2_send.at[h, k], recv_sem=p2_sem.at[h, k],
             device_id=(second[h] * 2 + core,), device_id_type=MESH)
 
@@ -112,8 +116,6 @@
             pltpu.make_async_copy(rx.at[h, kind, 0, rows], near0, load_sem.at[2]),
             pltpu.make_async_copy(rx.at[h, kind, 1, rows], near1, load_sem.at[3]),
         ]
-        if kind == 1:
-            copies.append(pltpu.make_async_copy(p2.at[h, rows], last, load_sem.at[4]))
         for copy in copies:
             copy.start()
         for copy in copies:
@@ -144,29 +146,45 @@
 
     for h in range(2):
         pair_copy(h, 1).wait_recv()
-        for from_core in range(2):
-            for k in range(directs):
-                rows = pl.ds(k * DIRECT, DIRECT)
-                pltpu.make_async_copy(rx.at[h, 1, from_core, rows], rx.at[h, 1, from_core, rows], direct_sem.at[h, from_core, k]).wait()
+
+    def own_step(k, carry):
+        for h in range(2):
+            loads(h, 1, k)
+
+            def add(group, carry):
+                base = pl.multiple_of(group * GROUP, GROUP)
+                mine[h, pl.ds(pl.multiple_of(k * CHUNK + base, GROUP), GROUP)] = four(pl.ds(base, GROUP))
+                return carry
+
+            lax.fori_loop(0, CHUNK // GROUP, add, 0)
+        return carry
+
+    for part in range(directs):
+        for h in range(2):
+            for from_core in range(2):
+                rows = pl.ds(part * DIRECT, DIRECT)
+                pltpu.make_async_copy(rx.at[h, 1, from_core, rows], rx.at[h, 1, from_core, rows], direct_sem.at[h, from_core, part]).wait()
+        lax.fori_loop(part * DIRECT // CHUNK, (part + 1) * DIRECT // CHUNK, own_step, 0)
 
     squares[...] = jnp.zeros_like(squares)
 
+    def store(h, k):
+        rows = pl.ds(k * CHUNK, CHUNK)
+        return pltpu.make_async_copy(mine.at[h, rows], total.at[pl.ds(h * half + k * CHUNK, CHUNK)], store_sem.at[h, k])
+
     def owner_step(k, carry):
         for h in range(2):
             second_copy(h, k).wait_recv()
-            loads(h, 1, k)
 
             def add(group, carry):
-                rows = pl.ds(pl.multiple_of(group * GROUP, GROUP), GROUP)
-                mean = (four(rows) + last[rows]) * (1.0 / count)
-                result[rows] = mean
+                rows = pl.ds(pl.multiple_of(k * CHUNK + group * GROUP, GROUP), GROUP)
+                mean = (mine[h, rows] + inbox[h, rows]) * (1.0 / count)
+                mine[h, rows] = mean
                 squares[...] += mean * mean
                 return carry
 
             lax.fori_loop(0, CHUNK // GROUP, add, 0)
-            store = pltpu.make_async_copy(result, total.at[pl.ds(h * half + k * CHUNK, CHUNK)], store_sem.at[0])
-            store.start()
-            store.wait()
+            store(h, k).start()
         return carry
 
     lax.fori_loop(0, chunks, owner_step, 0)
@@ -201,6 +219,9 @@
         pltpu.make_async_copy(norms.at[source], norms.at[source], norm_sem.at[source]).wait()
     for step in range(1, count):
         norm_copy(step).wait_send()
+    for h in range(2):
+        for k in range(chunks):
+            store(h, k).wait()
     square_sum = jnp.sum(jnp.sum(norms[...], axis=0))
     norm = jnp.sqrt(jnp.full(clip.shape, square_sum, jnp.float32))
     clip[...] = jnp.minimum(1.0, 1.0 / (norm + 1e-6))
@@ -220,18 +241,17 @@
             jax.ShapeDtypeStruct((8, 128), jnp.float32),
             jax.ShapeDtypeStruct((2, 2, 2, half, width), jnp.bfloat16),
             jax.ShapeDtypeStruct((2, 2, half, width), jnp.bfloat16),
-            jax.ShapeDtypeStruct((2, half, width), jnp.float32),
         ),
         in_specs=[any_space],
-        out_specs=(any_space, pl.BlockSpec(memory_space=pltpu.VMEM), any_space, any_space, any_space),
+        out_specs=(any_space, pl.BlockSpec(memory_space=pltpu.VMEM), any_space, any_space),
         scratch_shapes=[
+            pltpu.VMEM((2, half, width), jnp.float32),
+            pltpu.VMEM((2, half, width), jnp.float32),
             pltpu.VMEM((2, half, width), jnp.float32),
             pltpu.VMEM((CHUNK, width), jnp.bfloat16),
             pltpu.VMEM((CHUNK, width), jnp.bfloat16),
             pltpu.VMEM((CHUNK, width), jnp.bfloat16),
             pltpu.VMEM((CHUNK, width), jnp.bfloat16),
-            pltpu.VMEM((CHUNK, width), jnp.float32),
-            pltpu.VMEM((CHUNK, width), jnp.float32),
             pltpu.VMEM((GROUP, width), jnp.float32),
             pltpu.VMEM((count, 8, 128), jnp.float32),
             pltpu.SemaphoreType.DMA((2, 2, chunks)),
@@ -244,8 +264,8 @@
             pltpu.SemaphoreType.DMA((2, 2)),
             pltpu.SemaphoreType.DMA((2, chunks)),
             pltpu.SemaphoreType.DMA((count,)),
-            pltpu.SemaphoreType.DMA((5,)),
-            pltpu.SemaphoreType.DMA((1,)),
+            pltpu.SemaphoreType.DMA((4,)),
+            pltpu.SemaphoreType.DMA((2, chunks)),
         ],
         compiler_params=pltpu.CompilerParams(collective_id=0, has_side_effects=True, vmem_limit_bytes=60 * 1024 * 1024),
     )(local_grads.reshape(count, rows, width))
@@ -313,24 +333,172 @@
     )(*args)
 
 
-def place_kernel(gathered, working_in, working):
-    working[...] = gathered[0]
+def gather_kernel(rows, source, later_in, gathered, later, own, near_send, far_send, pair_send, near_sem, far_sem, pair_sem, load_sem, store_sem):
+    me, core, chip, x_near, y_near, diagonal = places("dp")
+    partner = chip * 2 + 1 - core
+    near = (x_near * 2 + core, y_near * 2 + core)
+    far = diagonal * 2 + core
+    half = rows // 2
+    steps = half // CHUNK
+
+    barrier = pltpu.get_barrier_semaphore()
+    for device in (partner, near[0], near[1]):
+        pl.semaphore_signal(barrier, inc=1, device_id=(device,), device_id_type=MESH)
+    pl.semaphore_wait(barrier, 3)
+
+    def span(h, k):
+        return pl.ds(h * half + k * CHUNK, CHUNK)
+
+    def near_copy(axis, h, k):
+        return pltpu.make_async_remote_copy(
+            src_ref=source.at[span(h, k)], dst_ref=gathered.at[me, span(h, k)],
+            send_sem=near_send.at[axis, h, k], recv_sem=near_sem.at[axis, h, k],
+            device_id=(near[axis],), device_id_type=MESH)
+
+    def far_copy(h, k):
+        return pltpu.make_async_remote_copy(
+            src_ref=gathered.at[near[h], span(h, k)], dst_ref=gathered.at[near[h], span(h, k)],
+            send_sem=far_send.at[h, k], recv_sem=far_sem.at[h, k],
+            device_id=(near[1 - h],), device_id_type=MESH)
+
+    def pair_copy(kind, h, k):
+        if kind == 0:
+            src, slab = source.at[span(h, k)], me
+        else:
+            slab = (near[0], near[1], far)[kind - 1]
+            src = gathered.at[slab, span(h, k)]
+        return pltpu.make_async_remote_copy(
+            src_ref=src, dst_ref=gathered.at[slab, span(h, k)],
+            send_sem=pair_send.at[kind, h, k], recv_sem=pair_sem.at[kind, h, k],
+            device_id=(partner,), device_id_type=MESH)
+
+    def arrived(slab, h, k, sem):
+        pltpu.make_async_copy(gathered.at[slab, span(h, k)], gathered.at[slab, span(h, k)], sem).wait()
+
+    for order in range(2):
+        for k in range(steps):
+            for axis in range(2):
+                near_copy(axis, axis if order == 0 else 1 - axis, k).start()
+    load = pltpu.make_async_copy(source, own, load_sem.at[0])
+    load.start()
+
+    def first_step(k, carry):
+        for h in range(2):
+            pair_copy(0, h, k).start()
+        for h in range(2):
+            arrived(near[h], h, k, near_sem.at[h, h, k])
+            far_copy(h, k).start()
+            pair_copy(1 + h, h, k).start()
+        return carry
+
+    lax.fori_loop(0, steps, first_step, 0)
+    load.wait()
+    store = pltpu.make_async_copy(own, gathered.at[me], store_sem.at[0])
+    store.start()
+
+    def second_step(k, carry):
+        for axis in range(2):
+            arrived(near[axis], 1 - axis, k, near_sem.at[axis, 1 - axis, k])
+            pair_copy(1 + axis, 1 - axis, k).start()
+        return carry
+
+    lax.fori_loop(0, steps, second_step, 0)
+
+    def third_step(k, carry):
+        for h in range(2):
+            arrived(far, h, k, far_sem.at[h, k])
+            pair_copy(3, h, k).start()
+        return carry
+
+    lax.fori_loop(0, steps, third_step, 0)
+    store.wait()
+
+    def finish(k, carry):
+        for h in range(2):
+            for axis in range(2):
+                near_copy(axis, h, k).wait_send()
+            far_copy(h, k).wait_send()
+            for kind in range(4):
+                pair_copy(kind, h, k).wait_send()
+            twin = (partner, x_near * 2 + 1 - core, y_near * 2 + 1 - core, diagonal * 2 + 1 - core)
+            for kind in range(4):
+                arrived(twin[kind], h, k, pair_sem.at[kind, h, k])
+        return carry
+
+    lax.fori_loop(0, steps, finish, 0)
+
+
+def gather_rows(block, later, count):
+    rows, width = block.shape
+    steps = rows // 2 // CHUNK
+    any_space = pl.BlockSpec(memory_space=pl.ANY)
+    return pl.pallas_call(
+        functools.partial(gather_kernel, rows),
+        name="gather_rows",
+        out_shape=(jax.ShapeDtypeStruct((count, rows, width), block.dtype), jax.ShapeDtypeStruct(later.shape, later.dtype)),
+        in_specs=[any_space, any_space],
+        out_specs=(any_space, any_space),
+        input_output_aliases={1: 1},
+        scratch_shapes=[
+            pltpu.VMEM((rows, width), block.dtype),
+            pltpu.SemaphoreType.DMA((2, 2, steps)),
+            pltpu.SemaphoreType.DMA((2, steps)),
+            pltpu.SemaphoreType.DMA((4, 2, steps)),
+            pltpu.SemaphoreType.DMA((2, 2, steps)),
+            pltpu.SemaphoreType.DMA((2, steps)),
+            pltpu.SemaphoreType.DMA((4, 2, steps)),
+            pltpu.SemaphoreType.DMA((1,)),
+            pltpu.SemaphoreType.DMA((1,)),
+        ],
+        cost_estimate=pl.CostEstimate(flops=40 * rows * width * count, bytes_accessed=4 * rows * width * count, transcendentals=0),
+        compiler_params=pltpu.CompilerParams(collective_id=1, has_side_effects=True, vmem_limit_bytes=60 * 1024 * 1024),
+    )(block, later)
+
+
+def place_kernel(start, gathered, working_in, working, ring, in_sem, out_sem):
+    count, rows, _ = gathered.shape
+    shard_rows = working.shape[0] // count
+    pieces = [(device, row) for row in range(0, rows, PIECE) for device in range(count)]
+
+    def read(i):
+        device, row = pieces[i]
+        return pltpu.make_async_copy(gathered.at[device, pl.ds(row, PIECE)], ring.at[i % DEPTH], in_sem.at[i % DEPTH])
+
+    def write(i):
+        device, row = pieces[i]
+        return pltpu.make_async_copy(ring.at[i % DEPTH], working.at[pl.ds(device * shard_rows + start + row, PIECE)], out_sem.at[i % DEPTH])
+
+    lead = DEPTH // 2
+    for i in range(len(pieces) + lead):
+        if i < len(pieces):
+            if i >= DEPTH:
+                write(i - DEPTH).wait()
+            read(i).start()
+        if i >= lead:
+            read(i - lead).wait()
+            write(i - lead).start()
+    for i in range(max(0, len(pieces) - DEPTH), len(pieces)):
+        write(i).wait()
 
 
 def place_rows(start, working, gathered):
     count, rows, width = gathered.shape
-    shard_rows = working.shape[0] // count
     size = rows * width * count
+    any_space = pl.BlockSpec(memory_space=pl.ANY)
     return pl.pallas_call(
-        place_kernel,
+        functools.partial(place_kernel, start),
         name="place_rows",
-        grid=(count, rows // 512),
         out_shape=jax.ShapeDtypeStruct(working.shape, working.dtype),
-        in_specs=[pl.BlockSpec((1, 512, width), lambda d, i: (d, i, 0)), pl.BlockSpec(memory_space=pl.ANY)],
-        out_specs=pl.BlockSpec((512, width), lambda d, i: (d * (shard_rows // 512) + start // 512 + i, 0)),
+        in_specs=[any_space, any_space],
+        out_specs=any_space,
         input_output_aliases={1: 0},
+        scratch_shapes=[
+            pltpu.VMEM((DEPTH, PIECE, width), working.dtype),
+            pltpu.SemaphoreType.DMA((DEPTH,)),
+            pltpu.SemaphoreType.DMA((DEPTH,)),
+        ],
         cost_estimate=pl.CostEstimate(flops=size, bytes_accessed=4 * size, transcendentals=0),
-        compiler_params=pltpu.CompilerParams(dimension_semantics=("arbitrary", "arbitrary")),
+        compiler_params=pltpu.CompilerParams(vmem_limit_bytes=48 * 1024 * 1024),
     )(gathered, working)
 
 
@@ -345,16 +513,20 @@
         rate = learn_rate.reshape(1)
         state = None
         start = 0
-        gathered = []
+        blocks = []
         for index, rows in enumerate(PARTS):
             shape = jax.ShapeDtypeStruct((total_rows, width), jnp.bfloat16) if index == len(PARTS) - 1 else None
             outs = update_rows(start, rows, runs, state, shape, rate, clip, grad, master, mom_first, mom_second)
             state = outs[0:3]
-            gathered.append((start, lax.all_gather(outs[3], "dp", axis=0, tiled=False)))
+            blocks.append(outs[3])
             start += rows
         working = outs[4]
-        for start, block in gathered:
-            working = place_rows(start, working, block)
+        early = lax.all_gather(blocks[0], "dp", axis=0, tiled=False)
+        middle, block = gather_rows(blocks[1], blocks[2], count)
+        late = lax.all_gather(block, "dp", axis=0, tiled=False)
+        working = place_rows(PARTS[0], working, middle)
+        working = place_rows(0, working, early)
+        working = place_rows(PARTS[0] + PARTS[1], working, late)
         return state[0], state[1], state[2], working
 
     return jax.shard_map(device_step, mesh=mesh, in_specs=(P("dp", None, None), P("dp", None), P("dp", None), P("dp", None), P()), out_specs=(P("dp", None), P("dp", None), P("dp", None), P(None, None)), check_vma=False)

time: 931 us -> 882 us (0.947)
  waiting for transfers between devices: 240 us -> 7.99 us
  Pallas kernels: 674 us -> 856 us
    all_gather x4 -> x2, waiting for transfers between devices: 240 us -> 7.96 us  [the longest x1 7.94 us: device_step(): late = lax.all_gather(block, 'dp', axis=0, tiled=False)]
    pallas_call x4, Pallas kernels: 69.8 us -> 259 us  [the longest x1 212 us: gather_rows(): pl.pallas_call(functools.partial(gather_kernel, rows), name='gather_rows'...]
    pallas_call x4 -> x3, Pallas kernels: 47.1 us -> 46.2 us  [update_rows(): pl.pallas_call(functools.partial(update_kernel, start, shard_rows, runs,...]
  transfers between devices with their start and end apart: 4 -> 2, of which waited for: 4 -> 1; matrix products, arithmetic and copies ran while one was open for 0% -> 0% of each run, Pallas kernels for 11% -> 33%
where the time goes in v2:
time: 882 us; the launch traced here: 881 us
  Pallas kernels  856 us (97%)
  between operations  14.8 us (2%)
    pallas_call x1, Pallas kernels, reduce_gradients(): pl.pallas_call(functools.partial(reduce_kernel, half), name='reduce_gradi...  551 us
    pallas_call x1, Pallas kernels, gather_rows(): pl.pallas_call(functools.partial(gather_kernel, rows), name='gather_rows'...  212 us
    pallas_call x3, Pallas kernels, place_rows(): pl.pallas_call(functools.partial(place_kernel, start), name='place_rows',...  47.1 us
    pallas_call x3, Pallas kernels, update_rows(): pl.pallas_call(functools.partial(update_kernel, start, shard_rows, runs,...  46.2 us
  transfers between devices with their start and end apart: 2, of which 1 were waited for; matrix products, arithmetic and copies ran while one was open for 0% of the time, Pallas kernels for 33%

profile of v2, /device:TPU:0, one launch (start us, length us, event | category | flops | bytes accessed | tf_op | source)
XLA Modules:
  0.0 880.5 jit_solution(10192162774571219536)
XLA Ops:
  7.2 0.0 all-gather.7.cloned.1.call-start
  7.2 551.1 %reduce_gradients.1 = (f32[4096,1024]{1,0:T(8,128)}, f32[8,128]{1,0:T(8,128)}, bf16[2,2,2,2048,1024]{4,3,2,1,0:T(8,128)(2,1)}, bf16[2,2,2048,1024]{3,2,1,0:T(8,128)(2,1)}) custom-call(bf16[8,4096,1024]{2,1,0:T(8,128)(2,1)} %bitcast.1.grads), custom_call_target="tpu_custom_call" | custom-call | tf_op jit(solution)/shard_map/reduce_gradients/pallas_call | solution.py:236
  559.0 0.0 copy-start.1
  559.0 0.7 copy-done.1
  559.6 0.0 copy-start.2
  559.6 6.2 update_rows.3
  565.9 0.0 all-gather.7.cloned.1.call-update
  565.9 0.0 all-gather.5.cloned.1.call-start
  565.9 0.0 copy-done.2
  565.9 33.9 %update_rows.4 = (f32[4096,1024]{1,0:T(8,128)}, f32[4096,1024]{1,0:T(8,128)}, f32[4096,1024]{1,0:T(8,128)}, bf16[3072,1024]{1,0:T(8,128)(2,1)}) custom-call(f32[1]{0:T(128)} %bitcast.5.learn_rate, f32[8,128]{1,0:T(8,128)S(1)} %copy-done.2, f32[4096,1024]{1,0:T(8,128)} %get-tuple-element.22.grad, ...), custom_call_target="tpu_custom_call", output_to_operand_aliasing={{0}: (6, {}), {1}: (7, {}), {2}: (8, {})} | custom-call | flops 62914560 | bytes 94371840 | tf_op jit(solution)/shard_map/update_rows/pallas_call | solution.py:323
  599.8 6.1 update_rows.5
  605.9 0.0 copy-start
  605.9 1.0 copy-done
  606.9 211.7 %gather_rows.1 = (bf16[8,3072,1024]{2,1,0:T(8,128)(2,1)}, bf16[512,1024]{1,0:T(8,128)(2,1)}) custom-call(bf16[3072,1024]{1,0:T(8,128)(2,1)} %get-tuple-element.32.source, bf16[512,1024]{1,0:T(8,128)(2,1)} %copy-done), custom_call_target="tpu_custom_call", output_to_operand_aliasing={{1}: (1, {})} | custom-call | flops 1006632960 | bytes 100663296 | tf_op jit(solution)/shard_map/gather_rows/pallas_call | solution.py:435
  818.6 0.0 all-gather.5.cloned.1.call-update
  818.6 33.9 %place_rows.3.working_in = bf16[32768,1024]{1,0:T(8,128)(2,1)} custom-call(bf16[8,3072,1024]{2,1,0:T(8,128)(2,1)} %get-tuple-element.36.gathered, bf16[32768,1024]{1,0:T(8,128)(2,1)} %get-tuple-element.37.working_in), custom_call_target="tpu_custom_call", output_to_operand_aliasing={{}: (1, {})} | custom-call | flops 25165824 | bytes 100663296 | tf_op jit(solution)/shard_map/place_rows/pallas_call | solution.py:488
  852.5 0.0 all-gather.7.cloned.1.call-done
  852.6 6.6 place_rows.4.working_in
  859.2 7.9 all-gather.5.cloned.1.call-done
  867.1 6.6 place_rows.5
Async XLA Ops:
  7.2 845.4 %all-gather.7.cloned.1.call-start = ((), (), s32[]{:S(2)}) async-start(), calls=%async_computation.1 | async-start | bytes 9437184 | tf_op jit(solution)/shard_map/all_gather | solution.py:524
  559.0 0.7 copy-start.1
  559.6 6.3 copy-start.2
  565.9 301.2 %all-gather.5.cloned.1.call-start = ((), (), s32[]{:S(2)}) async-start(), calls=%async_computation | async-start | bytes 9437184 | tf_op jit(solution)/shard_map/all_gather | solution.py:526
  605.9 1.0 copy-start
Sparse Core Ops, SparseCore 0:
  566.0 51.4 all-gather.6
  818.7 48.3 all-gather.4

commit v3 on v1

v3 whole, which is shorter than its diff:
```python
import functools

import jax
import jax.numpy as jnp
from jax import lax
from jax.experimental import pallas as pl
from jax.experimental.pallas import tpu as pltpu
from jax.sharding import PartitionSpec as P

LAYERS = 2
MIX_RANK = 32
DECAY_RANK = 64
ADAM_STEP = 10

MESH = pl.DeviceIdType.MESH
CHUNK = 256
DIRECT = 1024
GROUP = 16
TILE = 32
BLOCK = 256
LATE = 1024
PIECE = 512
DEPTH = 16


def layout_runs(model_width, total_rows):
    ffn_width = 7 * model_width // 2
    layer_rows = 6 * model_width + 2 * ffn_width + 16 + 10 * MIX_RANK + 2 * DECAY_RANK
    vocab_rows = (total_rows - LAYERS * layer_rows - 4) // 2
    base_rule = (1.0, 0.0)
    decay_rule = (1.0, 0.1)
    time_rule = (2.0, 0.0)
    pieces = [(vocab_rows, decay_rule)]
    for layer_idx in range(LAYERS):
        lead_rows = 12 if layer_idx == 0 else 10
        pieces = pieces + [(lead_rows + 10 * MIX_RANK, base_rule), (1, time_rule), (2 * DECAY_RANK, base_rule), (1, time_rule), (5 * model_width, decay_rule), (4, base_rule), (2 * ffn_width + model_width, decay_rule)]
    pieces = pieces + [(2, base_rule), (vocab_rows, decay_rule)]
    runs = []
    next_row = 0
    for run_len, run_rule in pieces:
        runs.append((next_row, run_rule[0], run_rule[1]))
        next_row = next_row + run_len
    return runs


def places(axis):
    me = lax.axis_index(axis)
    core, chip = lax.rem(me, 2), lax.div(me, 2)
    x, y = lax.rem(chip, 2), lax.div(chip, 2)
    return me, core, chip, y * 2 + 1 - x, (1 - y) * 2 + x, (1 - y) * 2 + 1 - x


def row_rules(base, rows, runs):
    row = base + lax.broadcasted_iota(jnp.int32, (rows, 128), 0)
    factor = jnp.full((rows, 128), runs[0][1], jnp.float32)
    decay = jnp.full((rows, 128), runs[0][2], jnp.float32)
    for before, run in zip(runs[:-1], runs[1:]):
        later = row >= run[0]
        if run[1] != before[1]:
            factor = jnp.where(later, run[1], factor)
        if run[2] != before[2]:
            decay = jnp.where(later, run[2], decay)
    return factor, decay


def adam(grad, scale, old, first, second, step_size, decay):
    clipped = grad * scale
    first_value = 0.9 * first + 0.1 * clipped
    second_value = 0.99 * second + 0.01 * (clipped * clipped)
    first_hat = first_value * (1.0 / (1.0 - 0.9 ** ADAM_STEP))
    second_hat = second_value * (1.0 / (1.0 - 0.99 ** ADAM_STEP))
    value = old - step_size * (first_hat / (jnp.sqrt(second_hat) + 1e-8) + decay * old)
    return value, first_value, second_value


def step_kernel(half, runs, learn_rate, grads, master, mom_first, mom_second, total, clip, rx, pd, stage, gathered, late,
                inbox, mine, own, other, near0, near1, tile, squares, norms, state, work,
                p1_send, direct_send, pair_send, p2_send, norm_send, rx_sem, direct_sem, pair_sem, p2_sem, norm_sem, load_sem, store_sem, stage_sem,
                state_sem, copy_sem, near_send, far_send, twin_send, near_sem, far_sem, twin_sem):
    me, core, chip, x_near, y_near, diagonal = places("dp")
    count = 8
    first = (x_near, y_near)
    second = (y_near, x_near)
    partner = chip * 2 + 1 - core
    chunks = half // CHUNK
    directs = half // DIRECT

    barrier = pltpu.get_barrier_semaphore()
    for step in range(1, count):
        pl.semaphore_signal(barrier, inc=1, device_id=(lax.rem(me + step, count),), device_id_type=MESH)
    pl.semaphore_wait(barrier, count - 1)

    def forward_copy(h, to_core, k):
        rows = pl.ds(h * half + k * CHUNK, CHUNK)
        return pltpu.make_async_remote_copy(
            src_ref=grads.at[diagonal * 2 + to_core, rows], dst_ref=rx.at[h, 0, core, pl.ds(k * CHUNK, CHUNK)],
            send_sem=p1_send.at[h, to_core, k], recv_sem=rx_sem.at[h, core, k],
            device_id=(first[h] * 2 + to_core,), device_id_type=MESH)

    def direct_copy(h, to_core, k):
        rows = pl.ds(h * half + k * DIRECT, DIRECT)
        return pltpu.make_async_remote_copy(
            src_ref=grads.at[first[h] * 2 + to_core, rows], dst_ref=rx.at[h, 1, core, pl.ds(k * DIRECT, DIRECT)],
            send_sem=direct_send.at[h, to_core, k], recv_sem=direct_sem.at[h, core, k],
            device_id=(first[h] * 2 + to_core,), device_id_type=MESH)

    def pair_copy(h, kind):
        owner = (second[h] if kind == 0 else chip) * 2 + 1 - core
        return pltpu.make_async_remote_copy(
            src_ref=grads.at[owner, pl.ds(h * half, half)], dst_ref=pd.at[h, kind],
            send_sem=pair_send.at[h, kind], recv_sem=pair_sem.at[h, kind],
            device_id=(partner,), device_id_type=MESH)

    def second_copy(h, k):
        rows = pl.ds(k * CHUNK, CHUNK)
        return pltpu.make_async_remote_copy(
            src_ref=stage.at[h, rows], dst_ref=inbox.at[h, rows],
            send_sem=p2_send.at[h, k], recv_sem=p2_sem.at[h, k],
            device_id=(second[h] * 2 + core,), device_id_type=MESH)

    for k in range(chunks):
        for h in range(2):
            for to_core in range(2):
                forward_copy(h, to_core, k).start()
        if k == 0:
            for h in range(2):
                pair_copy(h, 0).start()
        if k == 2:
            for h in range(2):
                pair_copy(h, 1).start()
    for k in range(directs):
        for h in range(2):
            for to_core in range(2):
                direct_copy(h, to_core, k).start()

    def loads(h, kind, k):
        owner = (second[h] if kind == 0 else chip) * 2 + core
        rows = pl.ds(k * CHUNK, CHUNK)
        copies = [
            pltpu.make_async_copy(grads.at[owner, pl.ds(h * half + k * CHUNK, CHUNK)], own, load_sem.at[0]),
            pltpu.make_async_copy(pd.at[h, kind, rows], other, load_sem.at[1]),
            pltpu.make_async_copy(rx.at[h, kind, 0, rows], near0, load_sem.at[2]),
            pltpu.make_async_copy(rx.at[h, kind, 1, rows], near1, load_sem.at[3]),
        ]
        for copy in copies:
            copy.start()
        for copy in copies:
            copy.wait()

    def four(rows):
        return (own[rows].astype(jnp.float32) + other[rows].astype(jnp.float32)) + (near0[rows].astype(jnp.float32) + near1[rows].astype(jnp.float32))

    for h in range(2):
        pair_copy(h, 0).wait_recv()

    def forward_step(k, carry):
        for h in range(2):
            for from_core in range(2):
                pltpu.make_async_copy(rx.at[h, 0, from_core, pl.ds(0, CHUNK)], rx.at[h, 0, from_core, pl.ds(0, CHUNK)], rx_sem.at[h, from_core, k]).wait()
            loads(h, 0, k)

            def add(group, carry):
                rows = pl.ds(pl.multiple_of(group * GROUP, GROUP), GROUP)
                tile[rows] = four(rows)
                return carry

            lax.fori_loop(0, CHUNK // GROUP, add, 0)
            put = pltpu.make_async_copy(tile, stage.at[h, pl.ds(k * CHUNK, CHUNK)], stage_sem.at[0])
            put.start()
            put.wait()
            second_copy(h, k).start()
        return carry

    lax.fori_loop(0, chunks, forward_step, 0)

    for h in range(2):
        pair_copy(h, 1).wait_recv()

    def own_step(k, carry):
        for h in range(2):
            loads(h, 1, k)

            def add(group, carry):
                base = pl.multiple_of(group * GROUP, GROUP)
                mine[pl.ds(pl.multiple_of(h * half + k * CHUNK + base, GROUP), GROUP)] = four(pl.ds(base, GROUP))
                return carry

            lax.fori_loop(0, CHUNK // GROUP, add, 0)
        return carry

    for part in range(directs):
        for h in range(2):
            for from_core in range(2):
                rows = pl.ds(part * DIRECT, DIRECT)
                pltpu.make_async_copy(rx.at[h, 1, from_core, rows], rx.at[h, 1, from_core, rows], direct_sem.at[h, from_core, part]).wait()
        lax.fori_loop(part * DIRECT // CHUNK, (part + 1) * DIRECT // CHUNK, own_step, 0)

    early = gathered.shape[1]
    span_rows = early // 2
    steps = span_rows // CHUNK
    late_steps = late.shape[0] // (2 * CHUNK)

    def early_row(h, k):
        return h * span_rows + k * CHUNK

    def late_row(h, k):
        return early + (2 * k + h) * CHUNK

    def state_copies(row, slot):
        return [pltpu.make_async_copy(source.at[pl.ds(row, CHUNK)], state.at[slot, i], state_sem.at[slot, i])
                for i, source in enumerate((master, mom_first, mom_second))]

    for h in range(2):
        for copy in state_copies(early_row(h, 0), h):
            copy.start()

    squares[...] = jnp.zeros_like(squares)

    def store(h, k):
        rows = pl.ds(h * half + k * CHUNK, CHUNK)
        return pltpu.make_async_copy(mine.at[rows], total.at[rows], store_sem.at[h, k])

    def owner_step(k, carry):
        for h in range(2):
            second_copy(h, k).wait_recv()

            def add(group, carry):
                base = pl.multiple_of(k * CHUNK + group * GROUP, GROUP)
                rows = pl.ds(pl.multiple_of(h * half + base, GROUP), GROUP)
                mean = (mine[rows] + inbox[h, pl.ds(base, GROUP)]) * (1.0 / count)
                mine[rows] = mean
                squares[...] += mean * mean
                return carry

            lax.fori_loop(0, CHUNK // GROUP, add, 0)
            store(h, k).start()
        return carry

    lax.fori_loop(0, chunks, owner_step, 0)

    lanes = jnp.sum(squares[...].reshape(GROUP // 8, 8, squares.shape[1]), axis=0)
    partial = lanes[:, 0:128]
    for column in range(1, squares.shape[1] // 128):
        partial += lanes[:, column * 128:(column + 1) * 128]
    norms[me] = partial

    def norm_copy(step):
        to = lax.rem(me + step, count)
        return pltpu.make_async_remote_copy(
            src_ref=norms.at[me], dst_ref=norms.at[me], send_sem=norm_send.at[step], recv_sem=norm_sem.at[me],
            device_id=(to,), device_id_type=MESH)

    for step in range(1, count):
        norm_copy(step).start()
    for step in range(1, count):
        source = lax.rem(me + step, count)
        pltpu.make_async_copy(norms.at[source], norms.at[source], norm_sem.at[source]).wait()
    square_sum = jnp.sum(jnp.sum(norms[...], axis=0))
    norm = jnp.sqrt(jnp.full(clip.shape, square_sum, jnp.float32))
    clip[...] = jnp.minimum(1.0, 1.0 / (norm + 1e-6))

    shard_rows = 2 * half
    near = (x_near * 2 + core, y_near * 2 + core)
    far = diagonal * 2 + core

    def span(h, k):
        return pl.ds(early_row(h, k), CHUNK)

    def near_copy(axis, h, k):
        return pltpu.make_async_remote_copy(
            src_ref=work.at[span(h, k)], dst_ref=gathered.at[me, span(h, k)],
            send_sem=near_send.at[axis, h, k], recv_sem=near_sem.at[axis, h, k],
            device_id=(near[axis],), device_id_type=MESH)

    def far_copy(h, k):
        return pltpu.make_async_remote_copy(
            src_ref=gathered.at[near[h], span(h, k)], dst_ref=gathered.at[near[h], span(h, k)],
            send_sem=far_send.at[h, k], recv_sem=far_sem.at[h, k],
            device_id=(near[1 - h],), device_id_type=MESH)

    def twin_copy(kind, h, k):
        if kind == 0:
            src, slab = work.at[span(h, k)], me
        else:
            slab = (near[0], near[1], far)[kind - 1]
            src = gathered.at[slab, span(h, k)]
        return pltpu.make_async_remote_copy(
            src_ref=src, dst_ref=gathered.at[slab, span(h, k)],
            send_sem=twin_send.at[kind, h, k], recv_sem=twin_sem.at[kind, h, k],
            device_id=(partner,), device_id_type=MESH)

    def arrived(slab, h, k, sem):
        pltpu.make_async_copy(gathered.at[slab, span(h, k)], gathered.at[slab, span(h, k)], sem).wait()

    def compute(row, slot, next_row):
        for copy in state_copies(row, slot):
            copy.wait()

        def update(group, carry):
            base = pl.multiple_of(group * TILE, TILE)
            here = pl.ds(base, TILE)
            there = pl.ds(pl.multiple_of(row + base, TILE), TILE)
            factor, decay = row_rules(me * shard_rows + row + base, TILE, runs)
            step_size = learn_rate[0] * factor
            for column in range(work.shape[1] // 128):
                lane = pl.ds(column * 128, 128)
                value = adam(mine[there, lane], clip[0:1, :], state[slot, 0, here, lane], state[slot, 1, here, lane], state[slot, 2, here, lane], step_size, decay)[0]
                work[there, lane] = value.astype(jnp.bfloat16)
            return carry

        lax.fori_loop(0, CHUNK // TILE, update, 0)
        if next_row is not None:
            for copy in state_copies(next_row, slot):
                copy.start()

    def early_step(k, carry):
        for h in range(2):
            compute(early_row(h, k), h, early_row(h, k + 1))
            near_copy(h, h, k).start()
            twin_copy(0, h, k).start()
        return carry

    lax.fori_loop(0, steps - 1, early_step, 0)
    for h in range(2):
        compute(early_row(h, steps - 1), h, late_row(h, 0))
        near_copy(h, h, steps - 1).start()
        twin_copy(0, h, steps - 1).start()

    def other_step(k, carry):
        for h in range(2):
            near_copy(1 - h, h, k).start()
        return carry

    lax.fori_loop(0, steps, other_step, 0)
    keep = pltpu.make_async_copy(work.at[pl.ds(0, early)], gathered.at[me], copy_sem.at[0])
    keep.start()

    def late_step(k, carry):
        for h in range(2):
            compute(late_row(h, k), h, late_row(h, k + 1))
        return carry

    lax.fori_loop(0, late_steps - 1, late_step, 0)
    for h in range(2):
        compute(late_row(h, late_steps - 1), h, None)
    leave = pltpu.make_async_copy(work.at[pl.ds(early, late.shape[0])], late, copy_sem.at[1])
    leave.start()

    def first_step(k, carry):
        for h in range(2):
            arrived(near[h], h, k, near_sem.at[h, h, k])
            far_copy(h, k).start()
            twin_copy(1 + h, h, k).start()
        return carry

    lax.fori_loop(0, steps, first_step, 0)

    def second_step(k, carry):
        for axis in range(2):
            arrived(near[axis], 1 - axis, k, near_sem.at[axis, 1 - axis, k])
            twin_copy(1 + axis, 1 - axis, k).start()
        return carry

    lax.fori_loop(0, steps, second_step, 0)

    def finish_reduce(k, carry):
        for h in range(2):
            for to_core in range(2):
                forward_copy(h, to_core, k).wait_send()
            second_copy(h, k).wait_send()
            store(h, k).wait()
        return carry

    lax.fori_loop(0, chunks, finish_reduce, 0)
    for h in range(2):
        for to_core in range(2):
            for k in range(directs):
                direct_copy(h, to_core, k).wait_send()
        for kind in range(2):
            pair_copy(h, kind).wait_send()
    for step in range(1, count):
        norm_copy(step).wait_send()
    keep.wait()
    leave.wait()

    def third_step(k, carry):
        for h in range(2):
            arrived(far, h, k, far_sem.at[h, k])
            twin_copy(3, h, k).start()
        return carry

    lax.fori_loop(0, steps, third_step, 0)

    def finish(k, carry):
        twin = (partner, x_near * 2 + 1 - core, y_near * 2 + 1 - core, diagonal * 2 + 1 - core)
        for h in range(2):
            for axis in range(2):
                near_copy(axis, h, k).wait_send()
            far_copy(h, k).wait_send()
            for kind in range(4):
                twin_copy(kind, h, k).wait_send()
                arrived(twin[kind], h, k, twin_sem.at[kind, h, k])
        return carry

    lax.fori_loop(0, steps, finish, 0)


def reduce_and_gather(local_grads, master, mom_first, mom_second, rate, runs, count):
    _, total_rows, width = local_grads.shape
    rows = total_rows // count
    half = rows // 2
    early = rows - LATE
    chunks, directs, steps = half // CHUNK, half // DIRECT, early // 2 // CHUNK
    any_space = pl.BlockSpec(memory_space=pl.ANY)
    dma = pltpu.SemaphoreType.DMA
    outs = pl.pallas_call(
        functools.partial(step_kernel, half, runs),
        name="reduce_and_gather",
        out_shape=(
            jax.ShapeDtypeStruct((rows, width), jnp.float32),
            jax.ShapeDtypeStruct((8, 128), jnp.float32),
            jax.ShapeDtypeStruct((2, 2, 2, half, width), jnp.bfloat16),
            jax.ShapeDtypeStruct((2, 2, half, width), jnp.bfloat16),
            jax.ShapeDtypeStruct((2, half, width), jnp.float32),
            jax.ShapeDtypeStruct((count, early, width), jnp.bfloat16),
            jax.ShapeDtypeStruct((LATE, width), jnp.bfloat16),
        ),
        in_specs=[pl.BlockSpec(memory_space=pltpu.SMEM)] + [any_space] * 4,
        out_specs=(any_space, pl.BlockSpec(memory_space=pltpu.VMEM)) + (any_space,) * 5,
        scratch_shapes=[
            pltpu.VMEM((2, half, width), jnp.float32),
            pltpu.VMEM((rows, width), jnp.float32),
            pltpu.VMEM((CHUNK, width), jnp.bfloat16),
            pltpu.VMEM((CHUNK, width), jnp.bfloat16),
            pltpu.VMEM((CHUNK, width), jnp.bfloat16),
            pltpu.VMEM((CHUNK, width), jnp.bfloat16),
            pltpu.VMEM((CHUNK, width), jnp.float32),
            pltpu.VMEM((GROUP, width), jnp.float32),
            pltpu.VMEM((count, 8, 128), jnp.float32),
            pltpu.VMEM((2, 3, CHUNK, width), jnp.float32),
            pltpu.VMEM((rows, width), jnp.bfloat16),
            dma((2, 2, chunks)), dma((2, 2, directs)), dma((2, 2)), dma((2, chunks)), dma((count,)),
            dma((2, 2, chunks)), dma((2, 2, directs)), dma((2, 2)), dma((2, chunks)), dma((count,)),
            dma((4,)), dma((2, chunks)), dma((1,)), dma((2, 3)), dma((2,)),
            dma((2, 2, steps)), dma((2, steps)), dma((4, 2, steps)), dma((2, 2, steps)), dma((2, steps)), dma((4, 2, steps)),
        ],
        compiler_params=pltpu.CompilerParams(collective_id=0, has_side_effects=True, vmem_limit_bytes=62 * 1024 * 1024),
    )(rate, local_grads.reshape(count, rows, width), master, mom_first, mom_second)
    return outs[0], outs[1], outs[5], outs[6]


def update_kernel(shard_rows, runs, learn_rate, clip, grad, master, first, second, new_master, new_first, new_second, working):
    block = grad.shape[0]
    factor, decay = row_rules(lax.axis_index("dp") * shard_rows + pl.program_id(0) * block, block, runs)
    step_size = learn_rate[0] * factor
    for column in range(grad.shape[1] // 128):
        lanes = pl.ds(column * 128, 128)
        value, first_value, second_value = adam(grad[:, lanes], clip[0:1, :], master[:, lanes], first[:, lanes], second[:, lanes], step_size, decay)
        new_master[:, lanes] = value
        new_first[:, lanes] = first_value
        new_second[:, lanes] = second_value


def update_rows(runs, count, learn_rate, clip, grad, master, first, second):
    shard_rows, width = grad.shape
    block = pl.BlockSpec((BLOCK, width), lambda i: (i, 0))
    whole = jax.ShapeDtypeStruct((shard_rows, width), jnp.float32)
    size = shard_rows * width
    return pl.pallas_call(
        functools.partial(update_kernel, shard_rows, runs),
        name="update_rows",
        grid=(shard_rows // BLOCK,),
        out_shape=(whole, whole, whole, jax.ShapeDtypeStruct((shard_rows * count, width), jnp.bfloat16)),
        in_specs=[pl.BlockSpec(memory_space=pltpu.SMEM), pl.BlockSpec((8, 128), lambda i: (0, 0)), block, block, block, block],
        out_specs=(block, block, block, pl.BlockSpec(memory_space=pl.ANY)),
        cost_estimate=pl.CostEstimate(flops=20 * size, bytes_accessed=28 * size, transcendentals=2 * size),
        compiler_params=pltpu.CompilerParams(dimension_semantics=("arbitrary",), vmem_limit_bytes=48 * 1024 * 1024),
    )(learn_rate, clip, grad, master, first, second)


def place_kernel(start, gathered, working_in, working, ring, in_sem, out_sem):
    count, rows, _ = gathered.shape
    shard_rows = working.shape[0] // count
    pieces = [(device, row) for row in range(0, rows, PIECE) for device in range(count)]

    def read(i):
        device, row = pieces[i]
        return pltpu.make_async_copy(gathered.at[device, pl.ds(row, PIECE)], ring.at[i % DEPTH], in_sem.at[i % DEPTH])

    def write(i):
        device, row = pieces[i]
        return pltpu.make_async_copy(ring.at[i % DEPTH], working.at[pl.ds(device * shard_rows + start + row, PIECE)], out_sem.at[i % DEPTH])

    lead = DEPTH // 2
    for i in range(len(pieces) + lead):
        if i < len(pieces):
            if i >= DEPTH:
                write(i - DEPTH).wait()
            read(i).start()
        if i >= lead:
            read(i - lead).wait()
            write(i - lead).start()
    for i in range(max(0, len(pieces) - DEPTH), len(pieces)):
        write(i).wait()


def place_rows(start, working, gathered):
    count, rows, width = gathered.shape
    size = rows * width * count
    any_space = pl.BlockSpec(memory_space=pl.ANY)
    return pl.pallas_call(
        functools.partial(place_kernel, start),
        name="place_rows",
        out_shape=jax.ShapeDtypeStruct(working.shape, working.dtype),
        in_specs=[any_space, any_space],
        out_specs=any_space,
        input_output_aliases={1: 0},
        scratch_shapes=[
            pltpu.VMEM((DEPTH, PIECE, width), working.dtype),
            pltpu.SemaphoreType.DMA((DEPTH,)),
            pltpu.SemaphoreType.DMA((DEPTH,)),
        ],
        cost_estimate=pl.CostEstimate(flops=size, bytes_accessed=4 * size, transcendentals=0),
        compiler_params=pltpu.CompilerParams(vmem_limit_bytes=48 * 1024 * 1024),
    )(gathered, working)


def solution(mesh):
    count = mesh.shape["dp"]

    def device_step(local_grads, master, mom_first, mom_second, learn_rate):
        shard_rows, width = master.shape
        total_rows = shard_rows * count
        runs = layout_runs(width, total_rows)
        rate = learn_rate.reshape(1)
        grad, clip, early, block = reduce_and_gather(local_grads, master, mom_first, mom_second, rate, runs, count)
        late = lax.all_gather(block, "dp", axis=0, tiled=False)
        new_master, new_first, new_second, working = update_rows(runs, count, rate, clip, grad, master, mom_first, mom_second)
        working = place_rows(0, working, early)
        working = place_rows(shard_rows - LATE, working, late)
        return new_master, new_first, new_second, working

    return jax.shard_map(device_step, mesh=mesh, in_specs=(P("dp", None, None), P("dp", None), P("dp", None), P("dp", None), P()), out_specs=(P("dp", None), P("dp", None), P("dp", None), P(None, None)), check_vma=False)
```

time: 931 us -> 874 us (0.939)
  waiting for transfers between devices: 240 us -> 7.7 us
  Pallas kernels: 674 us -> 850 us
    all_gather x4 -> x1, waiting for transfers between devices: 240 us -> 7.68 us  [device_step(): late = lax.all_gather(block, 'dp', axis=0, tiled=False)]
    pallas_call x9 -> x4, Pallas kernels: 674 us -> 850 us  [the longest x1 761 us: reduce_and_gather(): pl.pallas_call(functools.partial(step_kernel, half, runs), name='reduce_a...]
  transfers between devices with their start and end apart: 4 -> 1, of which waited for: 4 -> 1; matrix products, arithmetic and copies ran while one was open for 0% -> 0% of each run, Pallas kernels for 11% -> 9%
where the time goes in v3:
time: 874 us; the launch traced here: 873 us
  Pallas kernels  850 us (97%)
  between operations  14.7 us (2%)
    pallas_call x1, Pallas kernels, reduce_and_gather(): pl.pallas_call(functools.partial(step_kernel, half, runs), name='reduce_a...  761 us
    pallas_call x2, Pallas kernels, place_rows(): pl.pallas_call(functools.partial(place_kernel, start), name='place_rows',...  46.3 us
    pallas_call x1, Pallas kernels, update_rows(): pl.pallas_call(functools.partial(update_kernel, shard_rows, runs), name='...  42.3 us
  transfers between devices with their start and end apart: 1, of which 1 were waited for; matrix products, arithmetic and copies ran while one was open for 0% of the time, Pallas kernels for 9%

profile of v3, /device:TPU:0, one launch (start us, length us, event | category | flops | bytes accessed | tf_op | source)
XLA Modules:
  0.0 873.1 jit_solution(2011621010049071284)
XLA Ops:
  7.2 0.0 all-gather.3.cloned.1.call-start
  7.9 761.4 %reduce_and_gather.1 = (f32[4096,1024]{1,0:T(8,128)}, f32[8,128]{1,0:T(8,128)}, bf16[2,2,2,2048,1024]{4,3,2,1,0:T(8,128)(2,1)}, bf16[2,2,2048,1024]{3,2,1,0:T(8,...) custom-call(f32[1]{0:T(128)} %bitcast.3.learn_rate, ...), custom_call_target="tpu_custom_call" | custom-call | tf_op jit(solution)/shard_map/reduce_and_gather/pallas_call | solution.py:416
  769.3 0.0 all-gather.3.cloned.1.call-update
  769.3 0.0 copy-start
  769.3 0.7 copy-done
  770.0 42.3 %update_rows.1 = (f32[4096,1024]{1,0:T(8,128)}, f32[4096,1024]{1,0:T(8,128)}, f32[4096,1024]{1,0:T(8,128)}, bf16[32768,1024]{1,0:T(8,128)(2,1)}) custom-call(f32[1]{0:T(128)} %bitcast.4.learn_rate, f32[8,128]{1,0:T(8,128)S(1)} %copy-done, f32[4096,1024]{1,0:T(8,128)} %get-tuple-element.13.grad, f32[4096,1024]{1,0:T(8,128)} %master.3, f32[4096,1024]{1,0:T(8,128)} %first.1, ...), custom_call_target="tpu_custom_call" | custom-call | flops 83886080 | bytes 117440512 | tf_op jit(solution)/shard_map/update_rows/pallas_call | solution.py:469
  812.3 33.9 %place_rows.2.working_in = bf16[32768,1024]{1,0:T(8,128)(2,1)} custom-call(bf16[8,3072,1024]{2,1,0:T(8,128)(2,1)} %get-tuple-element.18.gathered, bf16[32768,1024]{1,0:T(8,128)(2,1)} %get-tuple-element.19.working_in), custom_call_target="tpu_custom_call", output_to_operand_aliasing={{}: (1, {})} | custom-call | flops 25165824 | bytes 100663296 | tf_op jit(solution)/shard_map/place_rows/pallas_call | solution.py:511
  846.2 7.7 all-gather.3.cloned.1.call-done
  853.9 12.4 %place_rows.3 = bf16[32768,1024]{1,0:T(8,128)(2,1)} custom-call(bf16[8,1024,1024]{2,1,0:T(8,128)(2,1)} %bitcast.5, bf16[32768,1024]{1,0:T(8,128)(2,1)} %place_rows.2.working_in), custom_call_target="tpu_custom_call", output_to_operand_aliasing={{}: (1, {})} | custom-call | flops 8388608 | bytes 33554432 | tf_op jit(solution)/shard_map/place_rows/pallas_call | solution.py:511
Async XLA Ops:
  7.2 846.7 %all-gather.3.cloned.1.call-start = ((), (), s32[]{:S(2)}) async-start(), calls=%async_computation | async-start | bytes 18874368 | tf_op jit(solution)/shard_map/all_gather | solution.py:537
  769.3 0.7 copy-start
Sparse Core Ops, SparseCore 0:
  769.4 84.4 all-gather.2
